TPU v7x, 128 devices: a whole 4x4x4 slice. The times are simulated.
128 devices in a mesh: gx: 8 (over x, core), gy: 16 (over y, z).
Axes of the slice: x: 4, y: 4, z: 4, core: 2. Of those that a mesh axis runs over, the one named last changes fastest.
Arguments:
- hot_ids: int32 [1048576], P(('gx', 'gy')), may hold values from 0 to 2047
- hot_grads: bfloat16 [1048576, 128], P(('gx', 'gy')), may hold values from -6 to 6
- cold_grads: bfloat16 [8, 16, 16, 512, 128], P('gx', 'gy'), may hold values from -6 to 6
- cold_slots: int32 [8, 16, 16, 512], P('gx', 'gy'), may hold values from 0 to 2047
- cold_counts: int32 [8, 16, 16], P('gx', 'gy'), may hold values from 1 to 512, as said below
Outputs:
- hot_grad: float32 [2048, 128], replicated
- cold_grad: float32 [8, 32768, 128], P('gx', 'gy')
Inputs may be any that keep to these rules, and one draw needn't show every extreme that they name: In each group g, some owner d receives cold_counts[g, s, d] = 512 from every s; loads per owner are skewed.
All inputs are finite; a program needn't handle non-finite values.
Results may differ from a plain program's by a relative error of at most 0.0003.
Values may be sent and summed in bfloat16 or wider, within the bound.
A program may use at most 64 MiB of HBM per device.

v0:
```python
import math

import jax
import jax.numpy as jnp
from jax import lax
from jax.sharding import PartitionSpec as P

HOT = 2048
OWN_ROWS = 2048


def split_up(array, dim, peers):
    dims = array.shape
    blocks = array.reshape(*dims[:dim], peers, dims[dim] // peers, *dims[dim + 1 :])
    return jnp.moveaxis(blocks, dim, 0)


def summed_on_arrival(array, axis, dim):
    blocks = split_up(array, dim, lax.axis_size(axis))
    arrived = lax.all_to_all(blocks, axis, split_axis=0, concat_axis=0, tiled=True)
    return arrived.sum(axis=0)


def gathered_total(array, axis):
    return lax.all_gather(array, axis).sum(0)


def laid_out(blocks, dim):
    blocks = jnp.moveaxis(blocks, 0, dim)
    dims = blocks.shape
    return blocks.reshape(*dims[:dim], dims[dim] * dims[dim + 1], *dims[dim + 2 :])


def sent_to_all(array, axis):
    peers = lax.axis_size(axis)
    return lax.all_to_all(
        jnp.broadcast_to(array[None], (peers, *array.shape)), axis, 0, 0, tiled=True
    )


def collect(array, axis, dim):
    return laid_out(sent_to_all(array, axis), dim)


def onehot_sum(row_ids, row_data, table_size, block_rows):
    turns = row_ids.shape[0] // block_rows
    id_blocks = row_ids.reshape(turns, block_rows)
    data_blocks = row_data.reshape(turns, block_rows, row_data.shape[1])
    table_iota = lax.broadcasted_iota(jnp.int32, (table_size, block_rows), 0)

    def add_block(total, pieces):
        ids_here, data_here = pieces
        selector = (table_iota == ids_here[None, :]).astype(jnp.bfloat16)
        return (total + jnp.dot(selector, data_here, preferred_element_type=jnp.float32), None)

    start = jnp.zeros((table_size, row_data.shape[1]), jnp.float32)
    total, unused = lax.scan(add_block, start, (id_blocks, data_blocks))
    return total


def hot_part(hot_ids, hot_grads):
    hot_rows = HOT
    block_rows = math.gcd(hot_ids.shape[0], 2048)
    local_sum = onehot_sum(hot_ids, hot_grads, hot_rows, block_rows)
    factor = (hot_rows / (hot_ids.shape[0] * lax.axis_size("gx") * lax.axis_size("gy"))) ** 0.5
    shared = summed_on_arrival(local_sum, "gy", 0)
    shared = gathered_total(shared, "gx")
    total = collect(shared, "gy", 0)
    return total * factor


def cold_part(cold_grads, cold_slots, cold_counts):
    owners, capacity, width = (cold_grads.shape[2], cold_grads.shape[3], cold_grads.shape[4])
    grads_here = cold_grads.reshape(owners, capacity, width)
    slots_here = cold_slots.reshape(owners, capacity)
    counts_here = cold_counts.reshape(owners)
    places = lax.broadcasted_iota(jnp.int32, (owners, capacity), 1)
    valid = places < counts_here[:, None]
    payload = jnp.where(valid[:, :, None], grads_here, jnp.zeros_like(grads_here))
    got_rows, got_slots = (
        lax.all_to_all(payload, "gy", split_axis=0, concat_axis=0, tiled=True),
        lax.all_to_all(slots_here, "gy", split_axis=0, concat_axis=0, tiled=True),
    )
    total_rows = owners * capacity
    block_rows = math.gcd(total_rows, 1024)
    table = onehot_sum(
        got_slots.reshape(total_rows), got_rows.reshape(total_rows, width), OWN_ROWS, block_rows
    )
    return table.reshape(1, OWN_ROWS, width)


def per_device(hot_ids, hot_grads, cold_grads, cold_slots, cold_counts):
    hot_grad = hot_part(hot_ids, hot_grads)
    cold_grad = cold_part(cold_grads, cold_slots, cold_counts)
    return (hot_grad, cold_grad)


def solution(mesh):
    return jax.shard_map(
        per_device,
        mesh=mesh,
        in_specs=(
            P(("gx", "gy")),
            P(("gx", "gy"), None),
            P("gx", "gy", None, None, None),
            P("gx", "gy", None, None),
            P("gx", "gy", None),
        ),
        out_specs=(P(), P("gx", "gy", None)),
        check_vma=False,
    )
```

profile of v0, /device:TPU:10, one launch (start us, length us, event | category | flops | bytes accessed | tf_op | source)
XLA Modules:
  0.0 120.6 jit_solution(17115255224648951507)
XLA Ops:
  0.6 1.4 %all_to_all.17 = s32[16,1,512]{2,1,0:T(1,128)} reshape(s32[1,1,16,512]{3,2,1,0:T(8,128)} %param.12) | data formatting | bytes 65536 | tf_op jit(solution)/shard_map/all_to_all | solution.py:82
  2.0 8.4 %all-to-all-start.2 = ((s32[16,1,512]{2,1,0:T(1,128)}), s32[16,1,512]{2,1,0:T(1,128)S(1)}, u32[]{:S(2)}, u32[]{:S(2)}) async-start(s32[16,1,512]{2,1,0:T(1,128)} %all_to_all.17), calls=%async_computation.2 | async-start | bytes 65536 | tf_op jit(solution)/shard_map/all_to_all | solution.py:82
  10.4 0.8 reshape.50
  11.2 17.6 %while.22 = (s32[]{:T(128)}, f32[2048,128]{1,0:T(8,128)S(1)}, s32[4,2048]{1,0:T(4,128)S(1)}, bf16[4,2048,128]{2,1,0:T(8,128)(2,1)}, s32[]{:T(128)}, /*index=5*/s32[]{:T(128)}) while((s32[]{:T(128)}, f32[2048,128]{1,0:T(8,128)S(1)}, s32[4,2048]{1,0:T(4,128)S(1)}, bf16[4,2048,128]{2,1,0:T(8,128)(2,1)}, s32[]{:T(128)}, ...), condition=%wide.region_1.2_spmd.clone, body=%wide.region_0.1_spmd.clone.sunk | while | flops 1078460416 | bytes 2646611 | solution.py:57
  11.2 4.4 %fusion.21 = f32[2048,128]{1,0:T(8,128)S(1)} fusion(s32[2048]{0:T(1024)S(1)} %bitcast.31, f32[2048,128]{1,0:T(8,128)S(1)} %get-tuple-element.165, bf16[4,2048,128]{2,1,0:T(8,128)(2,1)} %get-tuple-element.173, s32[]{:T(128)} %get-tuple-element.164, pred[]{:T(512)S(6)} %compare.6), kind=kOutput, calls=%fused_computation.5.clone.1 | convolution fusion | flops 1078460416 | bytes 2630145 | tf_op jit(solution)/shard_map/while/body/eval_jaxpr/dot_general | solution.py:54
  15.7 4.4 %fusion.21 = f32[2048,128]{1,0:T(8,128)S(1)} fusion(s32[2048]{0:T(1024)S(1)} %bitcast.31, f32[2048,128]{1,0:T(8,128)S(1)} %get-tuple-element.165, bf16[4,2048,128]{2,1,0:T(8,128)(2,1)} %get-tuple-element.173, s32[]{:T(128)} %get-tuple-element.164, pred[]{:T(512)S(6)} %compare.6), kind=kOutput, calls=%fused_computation.5.clone.1 | convolution fusion | flops 1078460416 | bytes 2630145 | tf_op jit(solution)/shard_map/while/body/eval_jaxpr/dot_general | solution.py:54
  20.1 4.4 %fusion.21 = f32[2048,128]{1,0:T(8,128)S(1)} fusion(s32[2048]{0:T(1024)S(1)} %bitcast.31, f32[2048,128]{1,0:T(8,128)S(1)} %get-tuple-element.165, bf16[4,2048,128]{2,1,0:T(8,128)(2,1)} %get-tuple-element.173, s32[]{:T(128)} %get-tuple-element.164, pred[]{:T(512)S(6)} %compare.6), kind=kOutput, calls=%fused_computation.5.clone.1 | convolution fusion | flops 1078460416 | bytes 2630145 | tf_op jit(solution)/shard_map/while/body/eval_jaxpr/dot_general | solution.py:54
  24.5 4.4 %fusion.21 = f32[2048,128]{1,0:T(8,128)S(1)} fusion(s32[2048]{0:T(1024)S(1)} %bitcast.31, f32[2048,128]{1,0:T(8,128)S(1)} %get-tuple-element.165, bf16[4,2048,128]{2,1,0:T(8,128)(2,1)} %get-tuple-element.173, s32[]{:T(128)} %get-tuple-element.164, pred[]{:T(512)S(6)} %compare.6), kind=kOutput, calls=%fused_computation.5.clone.1 | convolution fusion | flops 1078460416 | bytes 2630145 | tf_op jit(solution)/shard_map/while/body/eval_jaxpr/dot_general | solution.py:54
  28.8 0.0 copy-start.1
  28.8 0.0 copy-start.2
  28.9 0.0 copy-start
  28.9 0.0 all-to-all-done.2
  28.9 0.9 copy-done.1
  29.8 7.4 %all-to-all-start = ((f32[16,128,128]{2,1,0:T(8,128)}), f32[16,128,128]{2,1,0:T(8,128)S(1)}, u32[]{:S(2)}, u32[]{:S(2)}) async-start(f32[16,128,128]{2,1,0:T(8,128)} %bitcast.30), calls=%async_computation | async-start | bytes 2097152 | tf_op jit(solution)/shard_map/all_to_all | solution.py:20
  37.2 0.0 copy-done.2
  37.2 0.1 iota_compare_fusion.8
  37.2 0.0 copy-done
  37.3 2.7 %bitcast_select_fusion = bf16[16,512,128]{2,1,0:T(8,128)(2,1)} fusion(bf16[1,1,16,512,128]{4,3,2,1,0:T(8,128)(2,1)S(1)} %copy-done, pred[16,512]{1,0:T(8,128)(4,1)S(1)} %iota_compare_fusion.8), kind=kLoop, calls=%fused_computation.18 | loop fusion | flops 1048576 | bytes 4202496 | tf_op jit(solution)/shard_map/jit(_where)/select_n | solution.py:79
  40.0 12.0 %all-to-all-done = f32[16,128,128]{2,1,0:T(8,128)S(1)} async-done(((f32[16,128,128]{2,1,0:T(8,128)}), f32[16,128,128]{2,1,0:T(8,128)S(1)}, u32[]{:S(2)}, u32[]{:S(2)}) %all-to-all-start) | async-done | bytes 1048608 | tf_op jit(solution)/shard_map/all_to_all | solution.py:20
  51.9 5.8 %all-to-all-start.3 = ((bf16[16,512,128]{2,1,0:T(8,128)(2,1)}), bf16[16,512,128]{2,1,0:T(8,128)(2,1)S(1)}, u32[]{:S(2)}, u32[]{:S(2)}) async-start(bf16[16,512,128]{2,1,0:T(8,128)(2,1)} %bitcast_select_fusion), calls=%async_computation.3 | async-start | bytes 4194304 | tf_op jit(solution)/shard_map/all_to_all | solution.py:81
  57.7 0.1 reduce
  57.8 0.1 reduce_sum.18
  57.9 13.2 %all-gather = f32[1024,128]{1,0:T(8,128)S(1)} all-gather(f32[128,128]{1,0:T(8,128)S(1)} %reduce_sum.18), channel_id=2, replica_groups=mesh['gx'=8,'gy'=16] {'gx'}, dimensions={0}, use_global_device_ids=true | all-gather | bytes 589824 | tf_op jit(solution)/shard_map/all_gather | solution.py:25
  71.1 12.2 %all-to-all-done.3 = bf16[16,512,128]{2,1,0:T(8,128)(2,1)S(1)} async-done(((bf16[16,512,128]{2,1,0:T(8,128)(2,1)}), bf16[16,512,128]{2,1,0:T(8,128)(2,1)S(1)}, u32[]{:S(2)}, u32[]{:S(2)}) %all-to-all-start.3) | async-done | bytes 2097184 | tf_op jit(solution)/shard_map/all_to_all | solution.py:81
  83.2 1.1 broadcast_in_dim.10
  84.3 6.3 %all-to-all-start.1 = ((f32[16,128,128]{2,1,0:T(8,128)}), f32[16,128,128]{2,1,0:T(8,128)S(1)}, u32[]{:S(2)}, u32[]{:S(2)}) async-start(f32[16,128,128]{2,1,0:T(8,128)} %broadcast_in_dim.10), calls=%async_computation.1 | async-start | bytes 2097152 | tf_op jit(solution)/shard_map/all_to_all | solution.py:36
  90.7 28.8 %while.23 = (s32[]{:T(128)}, f32[2048,128]{1,0:T(8,128)}, s32[8,1024]{1,0:T(8,128)S(1)}, bf16[8,1024,128]{2,1,0:T(8,128)(2,1)S(1)}, s32[]{:T(128)}, /*index=5*/s32[]{:T(128)}) while((s32[]{:T(128)}, f32[2048,128]{1,0:T(8,128)}, s32[8,1024]{1,0:T(8,128)S(1)}, bf16[8,1024,128]{2,1,0:T(8,128)(2,1)S(1)}, s32[]{:T(128)}, ...), condition=%wide.region_5.6_spmd.clone, body=%wide.region_4.5_spmd.clone.sunk | while | flops 539492352 | bytes 2371671 | solution.py:57
  90.7 2.5 %fusion.23 = f32[2048,128]{1,0:T(8,128)} fusion(s32[1024]{0:T(1024)S(1)} %bitcast.32, f32[2048,128]{1,0:T(8,128)} %get-tuple-element.183, pred[]{:T(512)S(6)} %compare.7, bf16[8,1024,128]{2,1,0:T(8,128)(2,1)S(1)} %get-tuple-element.191, s32[]{:T(128)} %get-tuple-element.182), kind=kOutput, calls=%fused_computation.13.clone.1 | convolution fusion | flops 539492352 | bytes 2363397 | tf_op jit(solution)/shard_map/while/body/eval_jaxpr/dot_general | solution.py:54
  93.2 3.7 %fusion.23 = f32[2048,128]{1,0:T(8,128)} fusion(s32[1024]{0:T(1024)S(1)} %bitcast.32, f32[2048,128]{1,0:T(8,128)} %get-tuple-element.183, pred[]{:T(512)S(6)} %compare.7, bf16[8,1024,128]{2,1,0:T(8,128)(2,1)S(1)} %get-tuple-element.191, s32[]{:T(128)} %get-tuple-element.182), kind=kOutput, calls=%fused_computation.13.clone.1 | convolution fusion | flops 539492352 | bytes 2363397 | tf_op jit(solution)/shard_map/while/body/eval_jaxpr/dot_general | solution.py:54
  97.0 3.7 %fusion.23 = f32[2048,128]{1,0:T(8,128)} fusion(s32[1024]{0:T(1024)S(1)} %bitcast.32, f32[2048,128]{1,0:T(8,128)} %get-tuple-element.183, pred[]{:T(512)S(6)} %compare.7, bf16[8,1024,128]{2,1,0:T(8,128)(2,1)S(1)} %get-tuple-element.191, s32[]{:T(128)} %get-tuple-element.182), kind=kOutput, calls=%fused_computation.13.clone.1 | convolution fusion | flops 539492352 | bytes 2363397 | tf_op jit(solution)/shard_map/while/body/eval_jaxpr/dot_general | solution.py:54
  100.7 3.7 %fusion.23 = f32[2048,128]{1,0:T(8,128)} fusion(s32[1024]{0:T(1024)S(1)} %bitcast.32, f32[2048,128]{1,0:T(8,128)} %get-tuple-element.183, pred[]{:T(512)S(6)} %compare.7, bf16[8,1024,128]{2,1,0:T(8,128)(2,1)S(1)} %get-tuple-element.191, s32[]{:T(128)} %get-tuple-element.182), kind=kOutput, calls=%fused_computation.13.clone.1 | convolution fusion | flops 539492352 | bytes 2363397 | tf_op jit(solution)/shard_map/while/body/eval_jaxpr/dot_general | solution.py:54
  104.5 3.7 %fusion.23 = f32[2048,128]{1,0:T(8,128)} fusion(s32[1024]{0:T(1024)S(1)} %bitcast.32, f32[2048,128]{1,0:T(8,128)} %get-tuple-element.183, pred[]{:T(512)S(6)} %compare.7, bf16[8,1024,128]{2,1,0:T(8,128)(2,1)S(1)} %get-tuple-element.191, s32[]{:T(128)} %get-tuple-element.182), kind=kOutput, calls=%fused_computation.13.clone.1 | convolution fusion | flops 539492352 | bytes 2363397 | tf_op jit(solution)/shard_map/while/body/eval_jaxpr/dot_general | solution.py:54
  108.2 3.7 %fusion.23 = f32[2048,128]{1,0:T(8,128)} fusion(s32[1024]{0:T(1024)S(1)} %bitcast.32, f32[2048,128]{1,0:T(8,128)} %get-tuple-element.183, pred[]{:T(512)S(6)} %compare.7, bf16[8,1024,128]{2,1,0:T(8,128)(2,1)S(1)} %get-tuple-element.191, s32[]{:T(128)} %get-tuple-element.182), kind=kOutput, calls=%fused_computation.13.clone.1 | convolution fusion | flops 539492352 | bytes 2363397 | tf_op jit(solution)/shard_map/while/body/eval_jaxpr/dot_general | solution.py:54
  112.0 3.7 %fusion.23 = f32[2048,128]{1,0:T(8,128)} fusion(s32[1024]{0:T(1024)S(1)} %bitcast.32, f32[2048,128]{1,0:T(8,128)} %get-tuple-element.183, pred[]{:T(512)S(6)} %compare.7, bf16[8,1024,128]{2,1,0:T(8,128)(2,1)S(1)} %get-tuple-element.191, s32[]{:T(128)} %get-tuple-element.182), kind=kOutput, calls=%fused_computation.13.clone.1 | convolution fusion | flops 539492352 | bytes 2363397 | tf_op jit(solution)/shard_map/while/body/eval_jaxpr/dot_general | solution.py:54
  115.7 3.7 %fusion.23 = f32[2048,128]{1,0:T(8,128)} fusion(s32[1024]{0:T(1024)S(1)} %bitcast.32, f32[2048,128]{1,0:T(8,128)} %get-tuple-element.183, pred[]{:T(512)S(6)} %compare.7, bf16[8,1024,128]{2,1,0:T(8,128)(2,1)S(1)} %get-tuple-element.191, s32[]{:T(128)} %get-tuple-element.182), kind=kOutput, calls=%fused_computation.13.clone.1 | convolution fusion | flops 539492352 | bytes 2363397 | tf_op jit(solution)/shard_map/while/body/eval_jaxpr/dot_general | solution.py:54
  119.5 0.0 all-to-all-done.1
  119.5 1.1 broadcast_multiply_fusion
  (16 shorter events, 0.1 us)
Async XLA Ops:
  2.0 26.8 %all-to-all-start.2 = ((s32[16,1,512]{2,1,0:T(1,128)}), s32[16,1,512]{2,1,0:T(1,128)S(1)}, u32[]{:S(2)}, u32[]{:S(2)}) async-start(s32[16,1,512]{2,1,0:T(1,128)} %all_to_all.17), calls=%async_computation.2 | async-start | bytes 65536 | tf_op jit(solution)/shard_map/all_to_all | solution.py:82
  28.8 1.0 copy-start.1
  28.8 8.3 %copy-start.2 = (s32[1,1,16]{2,1,0:T(1,128)S(1)}, s32[1,1,16]{2,1,0:T(1,128)}, u32[]{:S(2)}) copy-start(s32[1,1,16]{2,1,0:T(1,128)} %param.13) | copy-start | bytes 196
  28.9 8.4 %copy-start = (bf16[1,1,16,512,128]{4,3,2,1,0:T(8,128)(2,1)S(1)}, bf16[1,1,16,512,128]{4,3,2,1,0:T(8,128)(2,1)}, u32[]{:S(2)}) copy-start(bf16[1,1,16,512,128]{4,3,2,1,0:T(8,128)(2,1)} %param.11) | copy-start | bytes 6291460
  29.8 22.1 %all-to-all-start = ((f32[16,128,128]{2,1,0:T(8,128)}), f32[16,128,128]{2,1,0:T(8,128)S(1)}, u32[]{:S(2)}, u32[]{:S(2)}) async-start(f32[16,128,128]{2,1,0:T(8,128)} %bitcast.30), calls=%async_computation | async-start | bytes 2097152 | tf_op jit(solution)/shard_map/all_to_all | solution.py:20
  51.9 31.3 %all-to-all-start.3 = ((bf16[16,512,128]{2,1,0:T(8,128)(2,1)}), bf16[16,512,128]{2,1,0:T(8,128)(2,1)S(1)}, u32[]{:S(2)}, u32[]{:S(2)}) async-start(bf16[16,512,128]{2,1,0:T(8,128)(2,1)} %bitcast_select_fusion), calls=%async_computation.3 | async-start | bytes 4194304 | tf_op jit(solution)/shard_map/all_to_all | solution.py:81
  84.3 35.2 %all-to-all-start.1 = ((f32[16,128,128]{2,1,0:T(8,128)}), f32[16,128,128]{2,1,0:T(8,128)S(1)}, u32[]{:S(2)}, u32[]{:S(2)}) async-start(f32[16,128,128]{2,1,0:T(8,128)} %broadcast_in_dim.10), calls=%async_computation.1 | async-start | bytes 2097152 | tf_op jit(solution)/shard_map/all_to_all | solution.py:36
where the time goes:
time: 122 us; the launch traced here: 121 us
  matrix products  46.1 us (38%)
  starting transfers between devices  27.9 us (23%)
  waiting for transfers between devices  24.2 us (20%)
  blocking collectives  13.2 us (11%)
  local copies, waits for them, and re-layouts  4.3 us (4%)
  other arithmetic  4.01 us (3%)
    dot_general x12, matrix products, add_block(): jnp.dot(selector, data_here, preferred_element_type=jnp.float32)  46.1 us
    all_gather x1, blocking collectives, gathered_total(): return lax.all_gather(array, axis).sum(0)  13.2 us
    all_to_all x1, waiting for transfers between devices, cold_part(): lax.all_to_all(payload, 'gy', split_axis=0, concat_axis=0, tiled=True)  12.2 us
    all_to_all x1, waiting for transfers between devices, summed_on_arrival(): lax.all_to_all(blocks, axis, split_axis=0, concat_axis=0, tiled=True)  12 us
    all_to_all x1, starting transfers between devices, cold_part(): lax.all_to_all(slots_here, 'gy', split_axis=0, concat_axis=0, tiled=True)  8.41 us
    all_to_all x1, starting transfers between devices, summed_on_arrival(): lax.all_to_all(blocks, axis, split_axis=0, concat_axis=0, tiled=True)  7.36 us
    all_to_all x1, starting transfers between devices, sent_to_all(): lax.all_to_all(jnp.broadcast_to(array[None], (peers, *array.shape)), axis...  6.33 us
    all_to_all x1, starting transfers between devices, cold_part(): lax.all_to_all(payload, 'gy', split_axis=0, concat_axis=0, tiled=True)  5.75 us
  transfers between devices with their start and end apart: 4, of which 2 were waited for; matrix products, arithmetic and copies ran while one was open for 41% of the time, Pallas kernels for 0%

commit v1 on v0

v1 whole, which is shorter than its diff:
```python
import jax
import jax.numpy as jnp
from jax import lax
from jax.experimental import pallas as pl
from jax.experimental.pallas import tpu as pltpu
from jax.sharding import PartitionSpec as P

MESH = pl.DeviceIdType.MESH
BF16 = jnp.bfloat16
F32 = jnp.float32

ROWS = 2048
HALF = 1024
WIDTH = 128
LOOK = 8192
CAP = 512
GX, GY, NX, NY, NZ = 8, 16, 4, 4, 4

NEAR = sorted(
    [(a, b) for a in range(NY) for b in range(NZ)],
    key=lambda o: (min(o[0], NY - o[0]) + min(o[1], NZ - o[1]), o),
)


def selector_tile(local_ref, row, base, iota):
    halves = []
    for side in range(2):
        ids = local_ref[pl.ds(row + side, 1), :] - base
        ids = jnp.broadcast_to(ids, (16, WIDTH)).astype(BF16)
        halves.append(
            jnp.concatenate(
                [
                    jnp.where(ids == (iota + BF16(16 * i)), BF16(1), BF16(0))
                    for i in range(16)
                ],
                axis=0,
            )
        )
    return jnp.concatenate(halves, axis=1)


def split_by_bit(bits_t, column, grads):
    high = grads * jnp.broadcast_to(bits_t[:, column : column + 1], (128, WIDTH)).astype(BF16)
    return grads - high, high


def kernel(
    ids_hbm, hot_hbm, cold_hbm, slots_hbm, counts,
    hot, cold,
    ids, grads, wide, local, slots, masked,
    partial, from_core, to_x, from_x, mine, from_y, got, got_slots, cold_local, cold_wide,
    local_sem, core_s, core_r, x_s, x_r, ys_s, ys_r, yg_s, yg_r,
    xg_s, xg_r, cg_s, cg_r, row_s, row_r, slot_s, slot_r,
):
    gx, gy = lax.axis_index("gx"), lax.axis_index("gy")
    x, core = gx // 2, lax.rem(gx, 2)
    y, z = gy // NZ, lax.rem(gy, NZ)

    def along_y(k):
        dy, dz = NEAR[k]
        return lax.rem(y + dy, NY) * NZ + lax.rem(z + dz, NZ)

    def x_peer(step):
        return lax.rem(x + step, NX)

    def at_gy(owner):
        return {"gx": gx, "gy": owner}

    def at_x(column):
        return {"gx": column * 2 + core, "gy": gy}

    other_core = {"gx": x * 2 + (1 - core), "gy": gy}

    def remote(src, dst, send, recv, where):
        return pltpu.make_async_remote_copy(
            src_ref=src, dst_ref=dst, send_sem=send, recv_sem=recv,
            device_id=where, device_id_type=MESH,
        )

    load_slots = pltpu.make_async_copy(slots_hbm, slots, local_sem.at[0])
    load_ids = pltpu.make_async_copy(ids_hbm, ids, local_sem.at[1])
    load_grads = pltpu.make_async_copy(hot_hbm, grads, local_sem.at[2])
    load_own = pltpu.make_async_copy(cold_hbm.at[gy], got.at[0], local_sem.at[3])
    load_slots.start()
    load_ids.start()
    load_grads.start()
    load_own.start()

    barrier = pltpu.get_barrier_semaphore()
    for k in range(1, GY):
        pl.semaphore_signal(barrier, inc=1, device_id=at_gy(along_y(k)), device_id_type=MESH)
    for step in range(1, NX):
        pl.semaphore_signal(barrier, inc=1, device_id=at_x(x_peer(step)), device_id_type=MESH)
    pl.semaphore_signal(barrier, inc=1, device_id=other_core, device_id_type=MESH)

    load_slots.wait()
    place = lax.broadcasted_iota(jnp.int32, (1, WIDTH), 1)
    masked[...] = jnp.full_like(masked, -1)
    for d in range(GY):
        for i in range(CAP // WIDTH):
            piece = slots[d : d + 1, i * WIDTH : (i + 1) * WIDTH]
            masked[d, i : i + 1, :] = jnp.where(place + i * WIDTH < counts[0, d], piece, -1)

    load_ids.wait()
    local[...] = (ids[...] & (HALF - 1)).astype(F32)
    bits_t = jnp.transpose((ids[...] >> 10).astype(F32))
    load_grads.wait()
    for r in range(LOOK // 128):
        rows = slice(r * 128, (r + 1) * 128)
        low, high = split_by_bit(bits_t, r, grads[rows, :])
        wide[rows, 0:WIDTH] = low
        wide[rows, WIDTH:] = high

    pl.semaphore_wait(barrier, GY - 1 + NX - 1 + 1)

    def row_copy(k):
        owner = along_y(k)
        return remote(cold_hbm.at[owner], got.at[k], row_s.at[k], row_r.at[k], at_gy(owner))

    def slot_copy(k):
        owner = along_y(k)
        return remote(masked.at[owner], got_slots.at[k], slot_s.at[k], slot_r.at[k], at_gy(owner))

    for k in range(1, GY):
        slot_copy(k).start()
        row_copy(k).start()

    iota = lax.broadcasted_iota(jnp.int32, (16, WIDTH), 0).astype(F32).astype(BF16)

    def core_copy(s):
        return remote(
            partial.at[s, 1 - core], from_core.at[s], core_s.at[s], core_r.at[s], other_core
        )

    def x_copy(s):
        return remote(to_x.at[s], from_x.at[s], x_s.at[s], x_r.at[s], at_x(x_peer(3 - s)))

    def hot_block(s, carry):
        base = (x_peer(3 - s) * 256).astype(F32)
        total = None
        for t in range(LOOK // 256):
            product = jnp.dot(
                selector_tile(local, 2 * t, base, iota),
                wide[t * 256 : (t + 1) * 256, :],
                preferred_element_type=F32,
            )
            total = product if total is None else total + product
        partial[s, 0] = total[:, :WIDTH]
        partial[s, 1] = total[:, WIDTH:]
        core_copy(s).start()

        @pl.when(s > 0)
        def _():
            core_copy(s - 1).wait_recv()
            to_x[s - 1] = partial[s - 1, core] + from_core[s - 1]
            x_copy(s - 1).start()

        return carry

    lax.fori_loop(0, NX, hot_block, 0)

    def cold_block(k, slot_rows, first):
        cold_local[...] = jnp.where(slot_rows < 0, -1, slot_rows & (HALF - 1)).astype(F32)
        turned = jnp.transpose((slot_rows >> 10).astype(F32))
        for r in range(CAP // 128):
            rows = slice(r * 128, (r + 1) * 128)
            low, high = split_by_bit(turned, r, got[k, rows, :])
            cold_wide[rows, 0:WIDTH] = low
            cold_wide[rows, WIDTH:] = high
        for j in range(4):
            total = None
            for t in range(CAP // 256):
                product = jnp.dot(
                    selector_tile(cold_local, 2 * t, 256.0 * j, iota),
                    cold_wide[t * 256 : (t + 1) * 256, :],
                    preferred_element_type=F32,
                )
                total = product if total is None else total + product
            rows = slice(j * 256, (j + 1) * 256)
            if first:
                cold[0, rows, :] = total[:, :WIDTH]
                cold[1, rows, :] = total[:, WIDTH:]
            else:
                cold[0, rows, :] += total[:, :WIDTH]
                cold[1, rows, :] += total[:, WIDTH:]

    def cold_blocks(low, high):
        def body(k, carry):
            remote(got.at[k], got.at[k], row_s.at[k], row_r.at[k], other_core).wait_recv()
            remote(
                got_slots.at[k], got_slots.at[k], slot_s.at[k], slot_r.at[k], other_core
            ).wait_recv()
            cold_block(k, got_slots[k], False)
            return carry

        lax.fori_loop(low, high, body, 0)

    load_own.wait()
    cold_block(0, masked[gy], True)

    core_copy(3).wait_recv()
    own = partial[3, core] + from_core[3]
    for s in range(3):
        x_copy(s).wait_recv()
        own = own + from_x[s]
    mine[...] = own.reshape(GY, 16, WIDTH)

    def scatter_copy(k):
        owner = along_y(k)
        return remote(mine.at[owner], from_y.at[k], ys_s.at[k], ys_r.at[k], at_gy(owner))

    for k in range(1, GY):
        scatter_copy(k).start()

    cold_blocks(1, 4)

    block = core * NX + x
    sum16 = mine[gy]
    for k in range(1, GY):
        scatter_copy(k).wait_recv()
        sum16 = sum16 + from_y[k]
    hot[block, gy] = sum16

    def gather_copy(k):
        return remote(
            hot.at[block, gy], hot.at[block, gy], yg_s.at[k], yg_r.at[k], at_gy(along_y(k))
        )

    for k in range(1, GY):
        gather_copy(k).start()

    cold_blocks(4, 7)

    for k in range(1, GY):
        gather_copy(k).wait_recv()

    def x_spread(step):
        return remote(
            hot.at[block], hot.at[block], xg_s.at[step], xg_r.at[step], at_x(x_peer(step))
        )

    def core_spread(step):
        piece = core * NX + x_peer(step)
        return remote(hot.at[piece], hot.at[piece], cg_s.at[step], cg_r.at[step], other_core)

    for step in range(1, NX):
        x_spread(step).start()
    core_spread(0).start()

    cold_blocks(7, 12)

    for step in range(1, NX):
        x_spread(step).wait_recv()
        piece = core * NX + x_peer(NX - step)
        remote(hot.at[piece], hot.at[piece], cg_s.at[step], cg_r.at[step], other_core).start()

    cold_blocks(12, GY)

    for step in range(NX):
        core_spread(step).wait_recv()

    for k in range(1, GY):
        slot_copy(k).wait_send()
        row_copy(k).wait_send()
        scatter_copy(k).wait_send()
        gather_copy(k).wait_send()
    for s in range(NX):
        core_copy(s).wait_send()
        core_spread(s).wait_send()
    for s in range(3):
        x_copy(s).wait_send()
        x_spread(s + 1).wait_send()


def per_device(hot_ids, hot_grads, cold_grads, cold_slots, cold_counts):
    factor = (ROWS / (LOOK * GX * GY)) ** 0.5
    in_hbm = pl.BlockSpec(memory_space=pltpu.HBM)
    in_vmem = pl.BlockSpec(memory_space=pltpu.VMEM)
    dma = pltpu.SemaphoreType.DMA
    hot, cold = pl.pallas_call(
        kernel,
        name="table_grads",
        out_shape=(
            jax.ShapeDtypeStruct((GX, GY, 16, WIDTH), F32),
            jax.ShapeDtypeStruct((2, HALF, WIDTH), F32),
        ),
        in_specs=[in_hbm] * 4 + [pl.BlockSpec(memory_space=pltpu.SMEM)],
        out_specs=[in_vmem] * 2,
        scratch_shapes=[
            pltpu.VMEM((LOOK // WIDTH, WIDTH), jnp.int32),
            pltpu.VMEM((LOOK, WIDTH), BF16),
            pltpu.VMEM((LOOK, 2 * WIDTH), BF16),
            pltpu.VMEM((LOOK // WIDTH, WIDTH), F32),
            pltpu.VMEM((GY, CAP), jnp.int32),
            pltpu.VMEM((GY, 8, WIDTH), jnp.int32),
            pltpu.VMEM((NX, 2, 256, WIDTH), F32),
            pltpu.VMEM((NX, 256, WIDTH), F32),
            pltpu.VMEM((3, 256, WIDTH), F32),
            pltpu.VMEM((3, 256, WIDTH), F32),
            pltpu.VMEM((GY, 16, WIDTH), F32),
            pltpu.VMEM((GY, 16, WIDTH), F32),
            pltpu.VMEM((GY, CAP, WIDTH), BF16),
            pltpu.VMEM((GY, 8, WIDTH), jnp.int32),
            pltpu.VMEM((8, WIDTH), F32),
            pltpu.VMEM((CAP, 2 * WIDTH), BF16),
            dma((4,)),
            dma((NX,)), dma((NX,)),
            dma((3,)), dma((3,)),
            dma((GY,)), dma((GY,)),
            dma((GY,)), dma((GY,)),
            dma((NX,)), dma((NX,)),
            dma((NX,)), dma((NX,)),
            dma((GY,)), dma((GY,)),
            dma((GY,)), dma((GY,)),
        ],
        compiler_params=pltpu.CompilerParams(
            collective_id=0, has_side_effects=True, vmem_limit_bytes=48 * 2**20
        ),
    )(
        hot_ids.reshape(LOOK // WIDTH, WIDTH),
        hot_grads,
        cold_grads.reshape(GY, CAP, WIDTH),
        cold_slots.reshape(GY, CAP),
        cold_counts.reshape(1, GY),
    )
    return hot.reshape(ROWS, WIDTH) * factor, cold.reshape(1, ROWS, WIDTH)


def solution(mesh):
    return jax.shard_map(
        per_device,
        mesh=mesh,
        in_specs=(
            P(("gx", "gy")),
            P(("gx", "gy"), None),
            P("gx", "gy", None, None, None),
            P("gx", "gy", None, None),
            P("gx", "gy", None),
        ),
        out_specs=(P(), P("gx", "gy", None)),
        check_vma=False,
    )
```

time: 122 us -> 61 us (0.50)
  the two profiles are of different devices: /device:TPU:10 before, /device:TPU:1 now
where the time goes in v1:
time: 61 us; the launch traced here: 60.5 us
  Pallas kernels  54.1 us (89%)
  local copies, waits for them, and re-layouts  4.72 us (8%)
  other arithmetic  1.06 us (2%)
  between operations  0.65 us (1%)
    pallas_call x1, Pallas kernels, per_device(): pl.pallas_call(kernel, name='table_grads', out_shape=(jax.ShapeDtypeStruc...  54.1 us
    unnamed x9, local copies, waits for them, and re-layouts  4.72 us

profile of v1, /device:TPU:1, one launch (start us, length us, event | category | flops | bytes accessed | tf_op | source)
XLA Modules:
  0.0 60.5 jit_solution(3216871434486626417)
XLA Ops:
  0.6 0.0 copy-start
  0.6 1.6 %copy-done = bf16[8192,128]{1,0:T(8,128)(2,1)S(1)} copy-done((bf16[8192,128]{1,0:T(8,128)(2,1)S(1)}, bf16[8192,128]{1,0:T(8,128)(2,1)}, u32[]{:S(2)}) %copy-start) | copy-done | bytes 2097176
  2.2 0.0 copy-start.1
  2.2 0.8 %copy-done.1 = s32[8192]{0:T(1024)S(1)} copy-done((s32[8192]{0:T(1024)S(1)}, s32[8192]{0:T(1024)}, u32[]{:S(2)}) %copy-start.1) | copy-done | bytes 32792
  3.0 0.0 copy-start.2
  3.0 0.8 %copy-done.2 = s32[1,1,16,512]{3,2,1,0:T(8,128)S(1)} copy-done((s32[1,1,16,512]{3,2,1,0:T(8,128)S(1)}, s32[1,1,16,512]{3,2,1,0:T(8,128)}, u32[]{:S(2)}) %copy-start.2) | copy-done | bytes 32792
  3.7 0.0 copy-start.3
  3.7 0.7 %copy-done.3 = s32[1,1,16]{2,1,0:T(1,128)S(1)} copy-done((s32[1,1,16]{2,1,0:T(1,128)S(1)}, s32[1,1,16]{2,1,0:T(1,128)}, u32[]{:S(2)}) %copy-start.3) | copy-done | bytes 88
  4.4 54.1 %table_grads.1 = (f32[8,16,16,128]{3,2,1,0:T(8,128)S(1)}, f32[2,1024,128]{2,1,0:T(8,128)S(1)}) custom-call(s32[64,128]{1,0:T(8,128)S(1)} %bitcast.7, bf16[8192,128]{1,0:T(8,128)(2,1)S(1)} %copy-done, bf16[16,512,128]{2,1,0:T(8,128)(2,1)} %bitcast.10, s32[16,512]{1,0:T(8,128)S(1)} %bitcast.8, s32[1,16]{1,0:T(1,128)S(1)} %bitcast.9), custom_call_target="tpu_custom_call" | custom-call | tf_op jit(solution)/shard_map/table_grads/pallas_call | solution.py:280
  58.5 1.1 %broadcast_multiply_fusion = f32[8,16,16,128]{3,2,1,0:T(8,128)} fusion(f32[8,16,16,128]{3,2,1,0:T(8,128)S(1)} %get-tuple-element.4), kind=kLoop, calls=%fused_computation | loop fusion | flops 262144 | bytes 2097152 | tf_op jit(solution)/shard_map/mul | solution.py:326
  59.6 1.0 %copy.8 = f32[1,2048,128]{2,1,0:T(8,128)} copy(f32[1,2048,128]{2,1,0:T(8,128)S(1)} %bitcast.6) | data formatting | bytes 2097152
Async XLA Ops:
  0.6 1.6 %copy-start = (bf16[8192,128]{1,0:T(8,128)(2,1)S(1)}, bf16[8192,128]{1,0:T(8,128)(2,1)}, u32[]{:S(2)}) copy-start(bf16[8192,128]{1,0:T(8,128)(2,1)} %hot_hbm.1) | copy-start | bytes 6291460
  2.2 0.8 %copy-start.1 = (s32[8192]{0:T(1024)S(1)}, s32[8192]{0:T(1024)}, u32[]{:S(2)}) copy-start(s32[8192]{0:T(1024)} %param.5) | copy-start | bytes 98308
  3.0 0.8 %copy-start.2 = (s32[1,1,16,512]{3,2,1,0:T(8,128)S(1)}, s32[1,1,16,512]{3,2,1,0:T(8,128)}, u32[]{:S(2)}) copy-start(s32[1,1,16,512]{3,2,1,0:T(8,128)} %param.8) | copy-start | bytes 98308
  3.7 0.7 %copy-start.3 = (s32[1,1,16]{2,1,0:T(1,128)S(1)}, s32[1,1,16]{2,1,0:T(1,128)}, u32[]{:S(2)}) copy-start(s32[1,1,16]{2,1,0:T(1,128)} %param.9) | copy-start | bytes 196

commit v2 on v1

--- a/solution.py
+++ b/solution.py
@@ -15,6 +15,8 @@
 LOOK = 8192
 CAP = 512
 GX, GY, NX, NY, NZ = 8, 16, 4, 4, 4
+WAVE1, WAVE2, C1, C2, C3 = 7, 10, 4, 7, 11
+FACTOR = (ROWS / (LOOK * GX * GY)) ** 0.5
 
 NEAR = sorted(
     [(a, b) for a in range(NY) for b in range(NZ)],
@@ -45,9 +47,9 @@
 
 
 def kernel(
-    ids_hbm, hot_hbm, cold_hbm, slots_hbm, counts,
+    ids_hbm, hot_hbm, cold_hbm, slots_hbm, counts_hbm,
     hot, cold,
-    ids, grads, wide, local, slots, masked,
+    ids, grads, wide, local, slots, counts, masked,
     partial, from_core, to_x, from_x, mine, from_y, got, got_slots, cold_local, cold_wide,
     local_sem, core_s, core_r, x_s, x_r, ys_s, ys_r, yg_s, yg_r,
     xg_s, xg_r, cg_s, cg_r, row_s, row_r, slot_s, slot_r,
@@ -81,6 +83,8 @@
     load_ids = pltpu.make_async_copy(ids_hbm, ids, local_sem.at[1])
     load_grads = pltpu.make_async_copy(hot_hbm, grads, local_sem.at[2])
     load_own = pltpu.make_async_copy(cold_hbm.at[gy], got.at[0], local_sem.at[3])
+    load_counts = pltpu.make_async_copy(counts_hbm, counts, local_sem.at[4])
+    load_counts.start()
     load_slots.start()
     load_ids.start()
     load_grads.start()
@@ -94,6 +98,7 @@
     pl.semaphore_signal(barrier, inc=1, device_id=other_core, device_id_type=MESH)
 
     load_slots.wait()
+    load_counts.wait()
     place = lax.broadcasted_iota(jnp.int32, (1, WIDTH), 1)
     masked[...] = jnp.full_like(masked, -1)
     for d in range(GY):
@@ -123,7 +128,12 @@
 
     for k in range(1, GY):
         slot_copy(k).start()
-        row_copy(k).start()
+
+    def send_rows(low, high):
+        for k in range(low, high):
+            row_copy(k).start()
+
+    send_rows(1, WAVE1)
 
     iota = lax.broadcasted_iota(jnp.int32, (16, WIDTH), 0).astype(F32).astype(BF16)
 
@@ -211,15 +221,16 @@
 
     for k in range(1, GY):
         scatter_copy(k).start()
-
-    cold_blocks(1, 4)
+    send_rows(WAVE1, WAVE2)
+
+    cold_blocks(1, C1)
 
     block = core * NX + x
     sum16 = mine[gy]
     for k in range(1, GY):
         scatter_copy(k).wait_recv()
         sum16 = sum16 + from_y[k]
-    hot[block, gy] = sum16
+    hot[block, gy] = sum16 * FACTOR
 
     def gather_copy(k):
         return remote(
@@ -228,8 +239,9 @@
 
     for k in range(1, GY):
         gather_copy(k).start()
-
-    cold_blocks(4, 7)
+    send_rows(WAVE2, GY)
+
+    cold_blocks(C1, C2)
 
     for k in range(1, GY):
         gather_copy(k).wait_recv()
@@ -247,14 +259,14 @@
         x_spread(step).start()
     core_spread(0).start()
 
-    cold_blocks(7, 12)
+    cold_blocks(C2, C3)
 
     for step in range(1, NX):
         x_spread(step).wait_recv()
         piece = core * NX + x_peer(NX - step)
         remote(hot.at[piece], hot.at[piece], cg_s.at[step], cg_r.at[step], other_core).start()
 
-    cold_blocks(12, GY)
+    cold_blocks(C3, GY)
 
     for step in range(NX):
         core_spread(step).wait_recv()
@@ -272,8 +284,18 @@
         x_spread(s + 1).wait_send()
 
 
+def store_tables(hot, cold, hot_out, cold_out, sem):
+    copies = [
+        pltpu.make_async_copy(hot, hot_out, sem.at[0]),
+        pltpu.make_async_copy(cold, cold_out, sem.at[1]),
+    ]
+    for copy in copies:
+        copy.start()
+    for copy in copies:
+        copy.wait()
+
+
 def per_device(hot_ids, hot_grads, cold_grads, cold_slots, cold_counts):
-    factor = (ROWS / (LOOK * GX * GY)) ** 0.5
     in_hbm = pl.BlockSpec(memory_space=pltpu.HBM)
     in_vmem = pl.BlockSpec(memory_space=pltpu.VMEM)
     dma = pltpu.SemaphoreType.DMA
@@ -284,7 +306,7 @@
             jax.ShapeDtypeStruct((GX, GY, 16, WIDTH), F32),
             jax.ShapeDtypeStruct((2, HALF, WIDTH), F32),
         ),
-        in_specs=[in_hbm] * 4 + [pl.BlockSpec(memory_space=pltpu.SMEM)],
+        in_specs=[in_hbm] * 5,
         out_specs=[in_vmem] * 2,
         scratch_shapes=[
             pltpu.VMEM((LOOK // WIDTH, WIDTH), jnp.int32),
@@ -292,6 +314,7 @@
             pltpu.VMEM((LOOK, 2 * WIDTH), BF16),
             pltpu.VMEM((LOOK // WIDTH, WIDTH), F32),
             pltpu.VMEM((GY, CAP), jnp.int32),
+            pltpu.SMEM((1, GY), jnp.int32),
             pltpu.VMEM((GY, 8, WIDTH), jnp.int32),
             pltpu.VMEM((NX, 2, 256, WIDTH), F32),
             pltpu.VMEM((NX, 256, WIDTH), F32),
@@ -303,7 +326,7 @@
             pltpu.VMEM((GY, 8, WIDTH), jnp.int32),
             pltpu.VMEM((8, WIDTH), F32),
             pltpu.VMEM((CAP, 2 * WIDTH), BF16),
-            dma((4,)),
+            dma((5,)),
             dma((NX,)), dma((NX,)),
             dma((3,)), dma((3,)),
             dma((GY,)), dma((GY,)),
@@ -317,13 +340,30 @@
             collective_id=0, has_side_effects=True, vmem_limit_bytes=48 * 2**20
         ),
     )(
-        hot_ids.reshape(LOOK // WIDTH, WIDTH),
-        hot_grads,
-        cold_grads.reshape(GY, CAP, WIDTH),
-        cold_slots.reshape(GY, CAP),
-        cold_counts.reshape(1, GY),
+        *(
+            pltpu.with_memory_space_constraint(a, pltpu.HBM)
+            for a in (
+                hot_ids.reshape(LOOK // WIDTH, WIDTH),
+                hot_grads,
+                cold_grads.reshape(GY, CAP, WIDTH),
+                cold_slots.reshape(GY, CAP),
+                cold_counts.reshape(1, GY),
+            )
+        )
     )
-    return hot.reshape(ROWS, WIDTH) * factor, cold.reshape(1, ROWS, WIDTH)
+    hot_grad, cold_grad = pl.pallas_call(
+        store_tables,
+        name="store_tables",
+        out_shape=(
+            jax.ShapeDtypeStruct((ROWS, WIDTH), F32),
+            jax.ShapeDtypeStruct((1, ROWS, WIDTH), F32),
+        ),
+        in_specs=[in_vmem] * 2,
+        out_specs=[in_hbm] * 2,
+        scratch_shapes=[dma((2,))],
+        compiler_params=pltpu.CompilerParams(vmem_limit_bytes=4 * 2**20),
+    )(hot.reshape(ROWS, WIDTH), cold.reshape(1, ROWS, WIDTH))
+    return hot_grad, cold_grad
 
 
 def solution(mesh):

time: 61 us -> 50.3 us (0.82)
  Pallas kernels: 54.1 us -> 49.1 us
  local copies, waits for them, and re-layouts: 4.72 us -> 0 us
  other arithmetic: 1.06 us -> 0 us
    pallas_call x1, Pallas kernels: 54.1 us -> 47.8 us  [per_device(): pl.pallas_call(kernel, name='table_grads', out_shape=(jax.ShapeDtypeStruc...]
    unnamed x9 -> x0, local copies, waits for them, and re-layouts: 4.72 us -> none
    pallas_call x0 -> x1, Pallas kernels: none -> 1.33 us  [per_device(): pl.pallas_call(store_tables, name='store_tables', out_shape=(jax.ShapeDty...]
    mul x1 -> x0, other arithmetic: 1.06 us -> none  [per_device(): return (hot.reshape(ROWS, WIDTH) * factor, cold.reshape(1, ROWS, WIDTH))]
where the time goes in v2:
time: 50.3 us; the launch traced here: 49.8 us
  Pallas kernels  49.1 us (98%)
  between operations  0.64 us (1%)
    pallas_call x1, Pallas kernels, per_device(): pl.pallas_call(kernel, name='table_grads', out_shape=(jax.ShapeDtypeStruc...  47.8 us
    pallas_call x1, Pallas kernels, per_device(): pl.pallas_call(store_tables, name='store_tables', out_shape=(jax.ShapeDty...  1.33 us

profile of v2, /device:TPU:1, one launch (start us, length us, event | category | flops | bytes accessed | tf_op | source)
XLA Modules:
  0.0 49.8 jit_solution(4623925490778934125)
XLA Ops:
  0.6 47.8 %table_grads.1 = (f32[8,16,16,128]{3,2,1,0:T(8,128)S(1)}, f32[2,1024,128]{2,1,0:T(8,128)S(1)}) custom-call(s32[64,128]{1,0:T(8,128)} %bitcast.9, bf16[8192,128]{1,0:T(8,128)(2,1)} %hot_hbm.1, bf16[16,512,128]{2,1,0:T(8,128)(2,1)} %bitcast.8, s32[16,512]{1,0:T(8,128)} %bitcast.10, s32[1,16]{1,0:T(1,128)} %bitcast.11), custom_call_target="tpu_custom_call" | custom-call | tf_op jit(solution)/shard_map/table_grads/pallas_call | solution.py:302
  48.4 1.3 %store_tables.1 = (f32[2048,128]{1,0:T(8,128)}, f32[1,2048,128]{2,1,0:T(8,128)}) custom-call(f32[2048,128]{1,0:T(8,128)S(1)} %bitcast.6, f32[1,2048,128]{2,1,0:T(8,128)S(1)} %bitcast.7), custom_call_target="tpu_custom_call" | custom-call | tf_op jit(solution)/shard_map/store_tables/pallas_call | solution.py:354

commit v3 on v2

--- a/solution.py
+++ b/solution.py
@@ -15,13 +15,10 @@
 LOOK = 8192
 CAP = 512
 GX, GY, NX, NY, NZ = 8, 16, 4, 4, 4
-WAVE1, WAVE2, C1, C2, C3 = 7, 10, 4, 7, 11
 FACTOR = (ROWS / (LOOK * GX * GY)) ** 0.5
 
-NEAR = sorted(
-    [(a, b) for a in range(NY) for b in range(NZ)],
-    key=lambda o: (min(o[0], NY - o[0]) + min(o[1], NZ - o[1]), o),
-)
+NEAR = [(0, 0), (1, 2), (3, 2), (2, 1), (2, 3), (2, 2), (0, 1), (0, 3), (1, 0), (3, 0), (1, 1), (3, 3), (1, 3), (3, 1), (0, 2), (2, 0)]
+WAVE1, WAVE2, C1, CA, C2, C3 = 6, 10, 1, 3, 6, 13
 
 
 def selector_tile(local_ref, row, base, iota):
@@ -65,6 +62,9 @@
     def x_peer(step):
         return lax.rem(x + step, NX)
 
+    def x_turn(s):
+        return x_peer(2 - s + s // 2 * 3 - s // 3 * 2)
+
     def at_gy(owner):
         return {"gx": gx, "gy": owner}
 
@@ -143,10 +143,10 @@
         )
 
     def x_copy(s):
-        return remote(to_x.at[s], from_x.at[s], x_s.at[s], x_r.at[s], at_x(x_peer(3 - s)))
+        return remote(to_x.at[s], from_x.at[s], x_s.at[s], x_r.at[s], at_x(x_turn(s)))
 
     def hot_block(s, carry):
-        base = (x_peer(3 - s) * 256).astype(F32)
+        base = (x_turn(s) * 256).astype(F32)
         total = None
         for t in range(LOOK // 256):
             product = jnp.dot(
@@ -239,9 +239,9 @@
 
     for k in range(1, GY):
         gather_copy(k).start()
+    cold_blocks(C1, CA)
     send_rows(WAVE2, GY)
-
-    cold_blocks(C1, C2)
+    cold_blocks(CA, C2)
 
     for k in range(1, GY):
         gather_copy(k).wait_recv()

time: 50.3 us -> 45.6 us (0.907)
  Pallas kernels: 49.1 us -> 44.3 us
    pallas_call x1, Pallas kernels: 47.8 us -> 43 us  [per_device(): pl.pallas_call(kernel, name='table_grads', out_shape=(jax.ShapeDtypeStruc...]
where the time goes in v3:
time: 45.6 us; the launch traced here: 45 us
  Pallas kernels  44.3 us (97%)
  between operations  0.64 us (1%)
    pallas_call x1, Pallas kernels, per_device(): pl.pallas_call(kernel, name='table_grads', out_shape=(jax.ShapeDtypeStruc...  43 us
    pallas_call x1, Pallas kernels, per_device(): pl.pallas_call(store_tables, name='store_tables', out_shape=(jax.ShapeDty...  1.33 us

profile of v3, /device:TPU:1, one launch (start us, length us, event | category | flops | bytes accessed | tf_op | source)
XLA Modules:
  0.0 45.0 jit_solution(14241450962192998851)
XLA Ops:
  0.6 43.0 %table_grads.1 = (f32[8,16,16,128]{3,2,1,0:T(8,128)S(1)}, f32[2,1024,128]{2,1,0:T(8,128)S(1)}) custom-call(s32[64,128]{1,0:T(8,128)} %bitcast.9, bf16[8192,128]{1,0:T(8,128)(2,1)} %hot_hbm.1, bf16[16,512,128]{2,1,0:T(8,128)(2,1)} %bitcast.8, s32[16,512]{1,0:T(8,128)} %bitcast.10, s32[1,16]{1,0:T(1,128)} %bitcast.11), custom_call_target="tpu_custom_call" | custom-call | tf_op jit(solution)/shard_map/table_grads/pallas_call | solution.py:302
  43.6 1.3 %store_tables.1 = (f32[2048,128]{1,0:T(8,128)}, f32[1,2048,128]{2,1,0:T(8,128)}) custom-call(f32[2048,128]{1,0:T(8,128)S(1)} %bitcast.6, f32[1,2048,128]{2,1,0:T(8,128)S(1)} %bitcast.7), custom_call_target="tpu_custom_call" | custom-call | tf_op jit(solution)/shard_map/store_tables/pallas_call | solution.py:354

commit v4 on v3

--- a/solution.py
+++ b/solution.py
@@ -18,7 +18,7 @@
 FACTOR = (ROWS / (LOOK * GX * GY)) ** 0.5
 
 NEAR = [(0, 0), (1, 2), (3, 2), (2, 1), (2, 3), (2, 2), (0, 1), (0, 3), (1, 0), (3, 0), (1, 1), (3, 3), (1, 3), (3, 1), (0, 2), (2, 0)]
-WAVE1, WAVE2, C1, CA, C2, C3 = 6, 10, 1, 3, 6, 13
+WAVE1, WAVE2, C1, CA, C2, C3 = 6, 10, 1, 5, 6, 14
 
 
 def selector_tile(local_ref, row, base, iota):
@@ -255,13 +255,13 @@
         piece = core * NX + x_peer(step)
         return remote(hot.at[piece], hot.at[piece], cg_s.at[step], cg_r.at[step], other_core)
 
-    for step in range(1, NX):
+    for step in (2, 1, 3):
         x_spread(step).start()
     core_spread(0).start()
 
     cold_blocks(C2, C3)
 
-    for step in range(1, NX):
+    for step in (1, 3, 2):
         x_spread(step).wait_recv()
         piece = core * NX + x_peer(NX - step)
         remote(hot.at[piece], hot.at[piece], cg_s.at[step], cg_r.at[step], other_core).start()

time: 45.6 us -> 45 us (0.987); the launches traced: 45 us -> 44.8 us
  no operation moved by 1% of the time
where the time goes in v4:
time: 45 us; the launch traced here: 44.8 us
  Pallas kernels  44.2 us (98%)
  between operations  0.64 us (1%)
    pallas_call x1, Pallas kernels, per_device(): pl.pallas_call(kernel, name='table_grads', out_shape=(jax.ShapeDtypeStruc...  42.8 us
    pallas_call x1, Pallas kernels, per_device(): pl.pallas_call(store_tables, name='store_tables', out_shape=(jax.ShapeDty...  1.33 us

profile of v4, /device:TPU:1, one launch (start us, length us, event | category | flops | bytes accessed | tf_op | source)
XLA Modules:
  0.0 44.8 jit_solution(15080382489871746600)
XLA Ops:
  0.6 42.8 %table_grads.1 = (f32[8,16,16,128]{3,2,1,0:T(8,128)S(1)}, f32[2,1024,128]{2,1,0:T(8,128)S(1)}) custom-call(s32[64,128]{1,0:T(8,128)} %bitcast.9, bf16[8192,128]{1,0:T(8,128)(2,1)} %hot_hbm.1, bf16[16,512,128]{2,1,0:T(8,128)(2,1)} %bitcast.8, s32[16,512]{1,0:T(8,128)} %bitcast.10, s32[1,16]{1,0:T(1,128)} %bitcast.11), custom_call_target="tpu_custom_call" | custom-call | tf_op jit(solution)/shard_map/table_grads/pallas_call | solution.py:302
  43.5 1.3 %store_tables.1 = (f32[2048,128]{1,0:T(8,128)}, f32[1,2048,128]{2,1,0:T(8,128)}) custom-call(f32[2048,128]{1,0:T(8,128)S(1)} %bitcast.6, f32[1,2048,128]{2,1,0:T(8,128)S(1)} %bitcast.7), custom_call_target="tpu_custom_call" | custom-call | tf_op jit(solution)/shard_map/store_tables/pallas_call | solution.py:354
